TPU v7x, 32 devices: a whole 2x2x4 slice. The times are simulated.
32 devices in a mesh: section: 8 (over z, x), dp: 4 (over y, core).
Axes of the slice: x: 2, y: 2, z: 4, core: 2. Of those that a mesh axis runs over, the one named last changes fastest.
Arguments:
- carry_act: bfloat16 [8, 32, 2304], P('section', 'dp'), may hold values from -6 to 6
- carry_act_tan: bfloat16 [8, 32, 2304], P('section', 'dp'), may hold values from -6 to 6
- carry_adj: bfloat16 [8, 32, 2304], P('section', 'dp'), may hold values from -0.75 to 0.75
- carry_adj_tan: bfloat16 [8, 32, 2304], P('section', 'dp'), may hold values from -0.75 to 0.75
- fresh_act: bfloat16 [2, 32, 2304], P(None, 'dp'), may hold values from -6 to 6
- loss_cot: bfloat16 [2, 32, 2304], P(None, 'dp'), may hold values from -0.75 to 0.75
- stash_act: bfloat16 [8, 2, 32, 2304], P('section', None, 'dp'), may hold values from -6 to 6
- stash_act_tan: bfloat16 [8, 2, 32, 2304], P('section', None, 'dp'), may hold values from -6 to 6
- norm_gain: bfloat16 [8, 2304], P('section'), may hold values from 0.25 to 1.75
- up_weight: bfloat16 [8, 2304, 4608], P('section', None, 'dp'), may hold values from -0.125 to 0.125
- down_weight: bfloat16 [8, 4608, 2304], P('section', 'dp'), may hold values from -0.09375 to 0.09375
- up_dir: bfloat16 [8, 2304, 4608], P('section', None, 'dp'), may hold values from -0.125 to 0.125
- down_dir: bfloat16 [8, 4608, 2304], P('section', 'dp'), may hold values from -0.09375 to 0.09375
Outputs:
- next_act: bfloat16 [8, 32, 2304], P('section', 'dp')
- next_act_tan: bfloat16 [8, 32, 2304], P('section', 'dp')
- next_adj: bfloat16 [8, 32, 2304], P('section', 'dp')
- next_adj_tan: bfloat16 [8, 32, 2304], P('section', 'dp')
- hvp_up: bfloat16 [8, 2304, 4608], P('section', None, 'dp')
- hvp_down: bfloat16 [8, 4608, 2304], P('section', 'dp')
All inputs are finite; a program needn't handle non-finite values.
Results may differ from a plain program's by a relative error of at most 0.02.
Values may be sent and summed in bfloat16 or wider, within the bound.
A program may use at most 128 MiB of HBM per device.

v0:
```python
import functools

import jax
import jax.numpy as jnp
from jax import lax
from jax.experimental import pallas as pl
from jax.experimental.pallas import tpu as pltpu
from jax.sharding import PartitionSpec as P

sqrt_two_over_pi = 0.7978845608028654
cubic_coef = 0.044715
norm_eps = 1e-06


def gelu_parts(linear):
    inner_arg = sqrt_two_over_pi * (linear + cubic_coef * linear * linear * linear)
    first_slope = sqrt_two_over_pi * (1.0 + 3.0 * cubic_coef * linear * linear)
    second_slope = 6.0 * sqrt_two_over_pi * cubic_coef * linear
    tanh_value = jnp.tanh(inner_arg)
    sech_square = 1.0 - tanh_value * tanh_value
    gelu_value = 0.5 * linear * (1.0 + tanh_value)
    gelu_first = 0.5 * (1.0 + tanh_value) + 0.5 * linear * sech_square * first_slope
    gelu_second = sech_square * (
        first_slope - linear * tanh_value * first_slope * first_slope + 0.5 * linear * second_slope
    )
    return (gelu_value, gelu_first, gelu_second)


def matrix_product(left, right):
    return jnp.dot(left, right, preferred_element_type=jnp.float32)


def product_last(left, right):
    return lax.dot_general(
        left, right, (((1,), (1,)), ((), ())), preferred_element_type=jnp.float32
    )


def product_first(left, right):
    return lax.dot_general(
        left, right, (((0,), (0,)), ((), ())), preferred_element_type=jnp.float32
    )


f32, bf16 = (jnp.float32, jnp.bfloat16)
MESH = pl.DeviceIdType.MESH


def lane_chunk(size, wanted):
    fits = [c for c in range(128, wanted + 1, 128) if size % c == 0]
    return max(fits) if fits else size


def over_chunks(size, chunk, body, after=None):
    count = size // chunk

    def step(index, carry):
        start = index * chunk if count == 1 else pl.multiple_of(index * chunk, chunk)
        body(pl.ds(start, chunk))
        if after is not None:
            after(index)
        return carry

    if count == 1:
        step(0, 0)
    else:
        lax.fori_loop(0, count, step, 0)


def once(index, wanted, work):
    if isinstance(index, int):
        if index == wanted:
            work()
    else:
        pl.when(index == wanted)(work)


def pair(value, tangent):
    blocks, rows, width = value.shape
    return jnp.stack([value, tangent], axis=1).reshape(blocks * 2 * rows, width)


def unpair(stacked, rows):
    wide = stacked.astype(f32).reshape(-1, 2, rows, stacked.shape[-1])
    return (wide[:, 0], wide[:, 1])


def norm_pair(stacked, gain, rows):
    values, values_tan = unpair(stacked, rows)
    inverse = lax.rsqrt(jnp.mean(values * values, axis=-1, keepdims=True) + norm_eps)
    inverse_tan = -(inverse * inverse * inverse) * jnp.mean(
        values * values_tan, axis=-1, keepdims=True
    )
    return (values * inverse * gain, (values_tan * inverse + values * inverse_tan) * gain)


def relay_kernel(
    sections, n_dp, ticks,
    carry_act, carry_act_tan, carry_adj, carry_adj_tan, fresh_act, loss_cot, stash_act,
    stash_act_tan, norm_gain, up_hbm, down_hbm, up_dir_hbm, down_dir_hbm,
    stash_out, adj_out, hidden_out, delta_out, final_out,
    up, down, up_dir, down_dir,
    left, left_dir, hid, hid_dir, slope, bend, hid_swap, delta, delta_dir, delta_swap,
    adj_dir, stash_all, gathered, outgoing, partial, from_core, to_chip, from_chip,
    weight_sems, out_sems, core_sems, chip_sems, shift_sems, relay_sems, stash_sems, stash_relay,
):
    chips = n_dp // 2
    rows = carry_act.shape[1]
    width = carry_act.shape[2]
    units = up.shape[1]
    band = n_dp * 2 * rows
    unit_chunk = lane_chunk(units, 384)
    width_chunk = lane_chunk(width, 768)
    pieces = width // width_chunk
    section, part = (lax.axis_index("section"), lax.axis_index("dp"))
    chip, core = (part // 2, part % 2)
    other = 1 - core
    after, before = (lax.rem(section + 1, sections), lax.rem(section + sections - 1, sections))
    partner = (section, chip * 2 + other)
    gain = norm_gain[...].astype(f32)

    def chip_at(step):
        return lax.rem(chip + step, chips)

    loads = [
        pltpu.make_async_copy(source.at[0], target, weight_sems.at[i])
        for i, (source, target) in enumerate(
            ((up_hbm, up), (up_dir_hbm, up_dir), (down_hbm, down), (down_dir_hbm, down_dir))
        )
    ]
    for load in loads:
        load.start()

    barrier = pltpu.get_barrier_semaphore()
    pl.semaphore_signal(barrier, inc=1, device_id=partner, device_id_type=MESH)
    for step in range(chips):
        place = chip_at(step) * 2 + core
        for where in (after, before):
            pl.semaphore_signal(barrier, inc=1, device_id=(where, place), device_id_type=MESH)
        if step:
            pl.semaphore_signal(barrier, inc=1, device_id=(section, place), device_id_type=MESH)

    def shift_copies(lane):
        where = after if lane % 2 == 0 else before
        return [
            pltpu.make_async_remote_copy(
                src_ref=outgoing.at[lane],
                dst_ref=gathered.at[lane, core, chip],
                send_sem=shift_sems.at[lane, 0, step],
                recv_sem=shift_sems.at[lane, 1, step],
                device_id=(where, chip_at(step) * 2 + core),
                device_id_type=MESH,
            )
            for step in range(chips)
        ]

    def relay_copy(lane):
        return pltpu.make_async_remote_copy(
            src_ref=gathered.at[lane, core],
            dst_ref=gathered.at[lane, core],
            send_sem=relay_sems.at[lane, 0],
            recv_sem=relay_sems.at[lane, 1],
            device_id=partner,
            device_id_type=MESH,
        )

    def stash_copies(tick):
        return [
            pltpu.make_async_remote_copy(
                src_ref=stash_all.at[tick, core, chip],
                dst_ref=stash_all.at[tick, core, chip],
                send_sem=stash_sems.at[tick, 0, step],
                recv_sem=stash_sems.at[tick, 1, step],
                device_id=(section, chip_at(step) * 2 + core),
                device_id_type=MESH,
            )
            for step in range(1, chips)
        ]

    def stash_relay_copy(tick):
        return pltpu.make_async_remote_copy(
            src_ref=stash_all.at[tick, core],
            dst_ref=stash_all.at[tick, core],
            send_sem=stash_relay.at[tick, 0],
            recv_sem=stash_relay.at[tick, 1],
            device_id=partner,
            device_id_type=MESH,
        )

    def relay_stash(tick):
        for copy in stash_copies(tick):
            copy.wait_recv()
        stash_relay_copy(tick).start()

    def columns(piece):
        if isinstance(piece, int):
            return pl.ds(piece * width_chunk, width_chunk)
        return pl.ds(pl.multiple_of(piece * width_chunk, width_chunk), width_chunk)

    def core_copy(lane, piece):
        return pltpu.make_async_remote_copy(
            src_ref=partial.at[lane, other, :, :, columns(piece)],
            dst_ref=from_core.at[lane, :, :, columns(piece)],
            send_sem=core_sems.at[lane, piece, 0],
            recv_sem=core_sems.at[lane, piece, 1],
            device_id=partner,
            device_id_type=MESH,
        )

    def chip_copies(lane, piece):
        return [
            pltpu.make_async_remote_copy(
                src_ref=to_chip.at[lane, step - 1, :, columns(piece)],
                dst_ref=from_chip.at[lane, step - 1, :, columns(piece)],
                send_sem=chip_sems.at[lane, piece, 0, step - 1],
                recv_sem=chip_sems.at[lane, piece, 1, step - 1],
                device_id=(section, chip_at(step) * 2 + core),
                device_id_type=MESH,
            )
            for step in range(1, chips)
        ]

    def start_all(copies):
        for copy in copies:
            copy.start()

    def stage_shift(lane, value, tangent):
        tick = lane // 2
        if lane % 2 == 0:
            ends, entering = (section == sections - 1, fresh_act[tick])
        else:
            ends, entering = (section == 0, loss_cot[tick])
        value = jnp.where(ends, entering.astype(f32), value)
        tangent = jnp.where(ends, 0.0, tangent)
        outgoing[lane] = pair(value[None], tangent[None]).astype(bf16)

    def relay(lane):
        for copy in shift_copies(lane):
            copy.wait_recv()
        relay_copy(lane).start()

    def reduce_in_chip(lane, piece):
        core_copy(lane, piece).wait_recv()
        cols = columns(piece)
        for step in range(1, chips):
            place = chip_at(step)
            summed = partial[lane, core, place, :, cols].astype(f32)
            summed = summed + from_core[lane, place, :, cols].astype(f32)
            to_chip[lane, step - 1, :, cols] = summed.astype(bf16)
        start_all(chip_copies(lane, piece))

    def reduced(lane):
        for piece in range(pieces):
            for copy in chip_copies(lane, piece):
                copy.wait_recv()
        total = partial[lane, core, chip].astype(f32) + from_core[lane, chip].astype(f32)
        for step in range(chips - 1):
            total = total + from_chip[lane, step].astype(f32)
        return (total[:rows], total[rows:])

    def norm_stash(tick):
        stacked = pair(
            stash_act[0, tick].astype(f32)[None], stash_act_tan[0, tick].astype(f32)[None]
        )
        normed, normed_tan = norm_pair(stacked, gain, rows)
        stash_all[tick, core, chip] = pair(normed, normed_tan).astype(bf16)

    stage_shift(0, carry_act[0].astype(f32), carry_act_tan[0].astype(f32))
    norm_stash(0)
    pl.semaphore_wait(barrier, 3 * chips)
    start_all(shift_copies(0))
    start_all(stash_copies(0))
    stage_shift(1, carry_adj[0].astype(f32), carry_adj_tan[0].astype(f32))
    for tick in range(1, ticks):
        norm_stash(tick)
    relay_stash(0)
    relay(0)
    start_all(shift_copies(1))
    for tick in range(1, ticks):
        start_all(stash_copies(tick))

    outs = []

    def send_out(source, target):
        copy = pltpu.make_async_copy(source, target, out_sems.at[len(outs)])
        copy.start()
        outs.append(copy)

    def stage_forward(tick):
        lane = 2 * tick
        relay_copy(lane).wait_recv()
        for block in range(n_dp):
            where = pl.ds(block * 2 * rows, 2 * rows)
            normed, normed_tan = norm_pair(
                gathered[lane, block // chips, block % chips], gain, rows
            )
            left[where, :] = pair(normed, normed_tan).astype(bf16)
            left_dir[where, :] = pair(jnp.zeros_like(normed), normed).astype(bf16)

    def stage_stash(tick):
        stash_relay_copy(tick).wait_recv()
        for block in range(n_dp):
            where = pl.ds(band + block * 2 * rows, 2 * rows)
            stacked = stash_all[tick, block // chips, block % chips]
            left[where, :] = stacked
            value = unpair(stacked, rows)[0]
            left_dir[where, :] = pair(jnp.zeros_like(value), value).astype(bf16)
        send_out(stash_all.at[tick], stash_out.at[tick])

    def up_products(forward, stash_tick, cols):
        low = 0 if forward else band
        high = band if stash_tick is None else 2 * band
        stacked = matrix_product(left[low:high, :], up[:, cols]) + matrix_product(
            left_dir[low:high, :], up_dir[:, cols]
        )
        if forward:
            linear, linear_tan = unpair(stacked[:band], rows)
            value, first, _ = gelu_parts(linear)
            hid[:, cols] = pair(value, first * linear_tan).astype(bf16)
            hid_dir[:, cols] = pair(jnp.zeros_like(value), value).astype(bf16)
        if stash_tick is not None:
            linear, linear_tan = unpair(stacked[band - low :], rows)
            value, first, second = gelu_parts(linear)
            hid_swap[stash_tick, :, cols] = pair(first * linear_tan, value).astype(bf16)
            slope[stash_tick, :, :, cols] = first
            bend[stash_tick, :, :, cols] = second * linear_tan

    def down_products(lane, cols):
        stacked = matrix_product(hid[...], down[:, cols]) + matrix_product(
            hid_dir[...], down_dir[:, cols]
        )
        partial[lane, :, :, :, cols] = stacked.astype(bf16).reshape(2, chips, 2 * rows, -1)

    def adjoint_products(tick, cols):
        adjoint = gathered[2 * tick + 1].reshape(band, width)
        stacked = product_last(adjoint, down[cols, :]) + product_last(
            adj_dir[...], down_dir[cols, :]
        )
        upstream, upstream_tan = unpair(stacked, rows)
        first, second_tan = (slope[tick, :, :, cols], bend[tick, :, :, cols])
        value = upstream * first
        tangent = upstream_tan * first + upstream * second_tan
        delta[:, cols] = pair(value, tangent).astype(bf16)
        delta_dir[:, cols] = pair(jnp.zeros_like(value), value).astype(bf16)
        delta_swap[tick, :, cols] = pair(tangent, value).astype(bf16)

    def back_products(lane, cols):
        stacked = product_last(delta[...], up[cols, :]) + product_last(
            delta_dir[...], up_dir[cols, :]
        )
        partial[lane, :, :, :, cols] = stacked.astype(bf16).reshape(2, chips, 2 * rows, -1)

    def finish_forward(tick):
        lane = 2 * tick
        value, tangent = reduced(lane)
        own = gathered[lane, core, chip].astype(f32)
        value, tangent = (own[:rows] + value, own[rows:] + tangent)
        if tick + 1 < ticks:
            stage_shift(lane + 2, value, tangent)
            start_all(shift_copies(lane + 2))
        else:
            final_out[0] = value.astype(bf16)
            final_out[1] = tangent.astype(bf16)

    def finish_backward(tick):
        lane = 2 * tick + 1
        summed, summed_tan = reduced(lane)
        arriving = gathered[lane, core, chip].astype(f32)
        values = stash_act[0, tick].astype(f32)
        values_tan = stash_act_tan[0, tick].astype(f32)
        inverse = lax.rsqrt(jnp.mean(values * values, axis=-1, keepdims=True) + norm_eps)
        cube = inverse * inverse * inverse
        inverse_tan = -cube * jnp.mean(values * values_tan, axis=-1, keepdims=True)
        weighted, weighted_tan = (summed * gain, summed_tan * gain)
        moment = jnp.mean(values * weighted, axis=-1, keepdims=True)
        moment_tan = jnp.mean(
            values_tan * weighted + values * weighted_tan, axis=-1, keepdims=True
        )
        value = arriving[:rows] + inverse * weighted - cube * values * moment
        tangent = (
            arriving[rows:]
            + inverse_tan * weighted
            + inverse * weighted_tan
            - 3.0 * inverse * inverse * inverse_tan * values * moment
            - cube * values_tan * moment
            - cube * values * moment_tan
        )
        if tick + 1 < ticks:
            stage_shift(lane + 2, value, tangent)
            start_all(shift_copies(lane + 2))
        else:
            final_out[2] = value.astype(bf16)
            final_out[3] = tangent.astype(bf16)

    def call(work, *given):
        return functools.partial(work, *given)

    def start_piece(lane, piece):
        core_copy(lane, piece).start()

    def stage_adjoint(tick):
        lane = 2 * tick + 1
        relay_copy(lane).wait_recv()
        for block in range(n_dp):
            value = unpair(gathered[lane, block // chips, block % chips], rows)[0]
            adj_dir[pl.ds(block * 2 * rows, 2 * rows), :] = pair(
                jnp.zeros_like(value), value
            ).astype(bf16)
        send_out(gathered.at[lane], adj_out.at[tick])

    stage_forward(0)
    stage_stash(0)
    loads[0].wait()
    loads[1].wait()
    last = pieces - 1
    for tick in range(ticks):
        ahead, behind = (2 * tick, 2 * tick + 1)
        if tick:
            stage_forward(tick)
        over_chunks(units, unit_chunk, call(up_products, True, None if tick else 0))
        if tick == 0:
            send_out(hid_swap.at[0], hidden_out.at[0])
            loads[2].wait()
            loads[3].wait()
        over_chunks(width, width_chunk, call(down_products, ahead), call(start_piece, ahead))
        relay(behind)
        stage_adjoint(tick)

        def reduce_pieces(index):
            def all_pieces():
                for piece in range(pieces):
                    reduce_in_chip(ahead, piece)

            once(index, 0, all_pieces)

        over_chunks(units, unit_chunk, call(adjoint_products, tick), reduce_pieces)
        send_out(delta_swap.at[tick], delta_out.at[tick])
        finish_forward(tick)
        if tick + 1 < ticks:
            relay_stash(tick + 1)

        def pass_piece(index):
            start_piece(behind, index)
            for piece in range(1, pieces):
                once(index, piece, call(reduce_in_chip, behind, piece - 1))

        over_chunks(width, width_chunk, call(back_products, behind), pass_piece)
        if tick + 1 < ticks:
            reduce_in_chip(behind, last)
            stage_stash(tick + 1)
            over_chunks(units, unit_chunk, call(up_products, False, tick + 1))
            send_out(hid_swap.at[tick + 1], hidden_out.at[tick + 1])
            relay(ahead + 2)
        else:
            reduce_in_chip(behind, last)
        finish_backward(tick)

    for lane in range(2 * ticks):
        for copy in shift_copies(lane):
            copy.wait_send()
        relay_copy(lane).wait_send()
        for piece in range(pieces):
            core_copy(lane, piece).wait_send()
            for copy in chip_copies(lane, piece):
                copy.wait_send()
    for tick in range(ticks):
        for copy in stash_copies(tick):
            copy.wait_send()
        stash_relay_copy(tick).wait_send()
    for copy in outs:
        copy.wait()


def curvature_kernel(
    stash_hbm, delta_hbm, hidden_hbm, adj_hbm, final_hbm,
    act, act_tan, adj_new, adj_new_tan, up_hbm, down_hbm,
    stash_sw, delta_sw, hidden_sw, adj, final, up_out, down_out, in_sems, row_sems, up_sems, down_sems,
):
    sources = (stash_hbm, delta_hbm, hidden_hbm, adj_hbm, final_hbm)
    targets = (stash_sw, delta_sw, hidden_sw, adj, final)
    loads = [
        pltpu.make_async_copy(source, target, in_sems.at[i])
        for i, (source, target) in enumerate(zip(sources, targets))
    ]
    for load in loads:
        load.start()
    for load in loads:
        load.wait()
    row_copies = [
        pltpu.make_async_copy(final.at[i], target.at[0], row_sems.at[i])
        for i, target in enumerate((act, act_tan, adj_new, adj_new_tan))
    ]
    for copy in row_copies:
        copy.start()

    def product(left, right, out, target, sems):
        chunk = out.shape[0] // sems.shape[0]

        def part(piece):
            where = pl.ds(piece * chunk, chunk)
            if not isinstance(piece, int):
                where = pl.ds(pl.multiple_of(piece * chunk, chunk), chunk)
            out[where, :] = product_first(left[:, where], right[...]).astype(bf16)
            copy = pltpu.make_async_copy(out.at[where, :], target.at[0, where, :], sems.at[piece])
            copy.start()

        return part

    up_part = product(stash_sw, delta_sw, up_out, up_hbm, up_sems)
    down_part = product(hidden_sw, adj, down_out, down_hbm, down_sems)
    if up_sems.shape[0] == down_sems.shape[0] > 1:

        def step(piece, carry):
            up_part(piece)
            down_part(piece)
            return carry

        lax.fori_loop(0, up_sems.shape[0], step, 0)
    else:
        for piece in range(up_sems.shape[0]):
            up_part(piece)
        for piece in range(down_sems.shape[0]):
            down_part(piece)
    for out, target, sems in ((up_out, up_hbm, up_sems), (down_out, down_hbm, down_sems)):
        chunk = out.shape[0] // sems.shape[0]
        for piece in range(sems.shape[0]):
            where = pl.ds(piece * chunk, chunk)
            pltpu.make_async_copy(out.at[where, :], target.at[0, where, :], sems.at[piece]).wait()
    for copy in row_copies:
        copy.wait()


def shards(
    carry_act, carry_act_tan, carry_adj, carry_adj_tan, fresh_act, loss_cot, stash_act,
    stash_act_tan, norm_gain, up_weight, down_weight, up_dir, down_dir,
):
    sections, n_dp = (lax.axis_size("section"), lax.axis_size("dp"))
    chips = n_dp // 2
    ticks, rows, width = fresh_act.shape
    units = up_weight.shape[2]
    band = n_dp * 2 * rows
    tall = 2 * band
    pieces = width // lane_chunk(width, 768)
    lanes = 2 * ticks
    vmem, anywhere = (
        pl.BlockSpec(memory_space=pltpu.VMEM),
        pl.BlockSpec(memory_space=pl.ANY),
    )
    block = (2 * rows, width)
    stash_out, adj_out, hidden_out, delta_out, final_out = pl.pallas_call(
        functools.partial(relay_kernel, sections, n_dp, ticks),
        out_shape=(
            jax.ShapeDtypeStruct((ticks, 2, chips) + block, bf16),
            jax.ShapeDtypeStruct((ticks, 2, chips) + block, bf16),
            jax.ShapeDtypeStruct((ticks, band, units), bf16),
            jax.ShapeDtypeStruct((ticks, band, units), bf16),
            jax.ShapeDtypeStruct((4, rows, width), bf16),
        ),
        in_specs=[vmem] * 9 + [anywhere] * 4,
        out_specs=(anywhere,) * 4 + (vmem,),
        scratch_shapes=[
            pltpu.VMEM((width, units), bf16),
            pltpu.VMEM((units, width), bf16),
            pltpu.VMEM((width, units), bf16),
            pltpu.VMEM((units, width), bf16),
            pltpu.VMEM((tall, width), bf16),
            pltpu.VMEM((tall, width), bf16),
            pltpu.VMEM((band, units), bf16),
            pltpu.VMEM((band, units), bf16),
            pltpu.VMEM((ticks, n_dp, rows, units), f32),
            pltpu.VMEM((ticks, n_dp, rows, units), f32),
            pltpu.VMEM((ticks, band, units), bf16),
            pltpu.VMEM((band, units), bf16),
            pltpu.VMEM((band, units), bf16),
            pltpu.VMEM((ticks, band, units), bf16),
            pltpu.VMEM((band, width), bf16),
            pltpu.VMEM((ticks, 2, chips) + block, bf16),
            pltpu.VMEM((lanes, 2, chips) + block, bf16),
            pltpu.VMEM((lanes,) + block, bf16),
            pltpu.VMEM((lanes, 2, chips) + block, bf16),
            pltpu.VMEM((lanes, chips) + block, bf16),
            pltpu.VMEM((lanes, chips - 1) + block, bf16),
            pltpu.VMEM((lanes, chips - 1) + block, bf16),
            pltpu.SemaphoreType.DMA((4,)),
            pltpu.SemaphoreType.DMA((4 * ticks,)),
            pltpu.SemaphoreType.DMA((lanes, pieces, 2)),
            pltpu.SemaphoreType.DMA((lanes, pieces, 2, chips - 1)),
            pltpu.SemaphoreType.DMA((lanes, 2, chips)),
            pltpu.SemaphoreType.DMA((lanes, 2)),
            pltpu.SemaphoreType.DMA((ticks, 2, chips)),
            pltpu.SemaphoreType.DMA((ticks, 2)),
        ],
        compiler_params=pltpu.CompilerParams(
            collective_id=0, has_side_effects=True, vmem_limit_bytes=60 * 1024 * 1024
        ),
        name="relay",
    )(
        carry_act, carry_act_tan, carry_adj, carry_adj_tan, fresh_act, loss_cot, stash_act,
        stash_act_tan, norm_gain, up_weight, down_weight, up_dir, down_dir,
    )
    deep = band * ticks
    stash_sw = stash_out.reshape(deep, width)
    delta_sw = delta_out.reshape(deep, units)
    hidden_sw = hidden_out.reshape(deep, units)
    adj_flat = adj_out.reshape(deep, width)
    rows_shape = jax.ShapeDtypeStruct((1, rows, width), bf16)
    return tuple(
        pl.pallas_call(
            curvature_kernel,
            out_shape=(rows_shape,) * 4
            + (
                jax.ShapeDtypeStruct((1, width, units), bf16),
                jax.ShapeDtypeStruct((1, units, width), bf16),
            ),
            in_specs=[anywhere] * 5,
            out_specs=(anywhere,) * 6,
            scratch_shapes=[
                pltpu.VMEM((deep, width), bf16),
                pltpu.VMEM((deep, units), bf16),
                pltpu.VMEM((deep, units), bf16),
                pltpu.VMEM((deep, width), bf16),
                pltpu.VMEM((4, rows, width), bf16),
                pltpu.VMEM((width, units), bf16),
                pltpu.VMEM((units, width), bf16),
                pltpu.SemaphoreType.DMA((5,)),
                pltpu.SemaphoreType.DMA((4,)),
                pltpu.SemaphoreType.DMA((width // lane_chunk(width, 768),)),
                pltpu.SemaphoreType.DMA((units // lane_chunk(units, 384),)),
            ],
            compiler_params=pltpu.CompilerParams(vmem_limit_bytes=60 * 1024 * 1024),
            name="curvature",
        )(stash_sw, delta_sw, hidden_sw, adj_flat, final_out)
    )


def solution(mesh):
    in_specs = (
        P("section", "dp", None),
        P("section", "dp", None),
        P("section", "dp", None),
        P("section", "dp", None),
        P(None, "dp", None),
        P(None, "dp", None),
        P("section", None, "dp", None),
        P("section", None, "dp", None),
        P("section", None),
        P("section", None, "dp"),
        P("section", "dp", None),
        P("section", None, "dp"),
        P("section", "dp", None),
    )
    out_specs = (
        P("section", "dp", None),
        P("section", "dp", None),
        P("section", "dp", None),
        P("section", "dp", None),
        P("section", None, "dp"),
        P("section", "dp", None),
    )
    return jax.shard_map(shards, mesh=mesh, in_specs=in_specs, out_specs=out_specs, check_vma=False)
```

profile of v0, /device:TPU:0, one launch (start us, length us, event | category | flops | bytes accessed | tf_op | source)
XLA Modules:
  0.0 62.9 jit_solution(7286620092923565976)
XLA Ops:
  0.6 56.0 %relay.1 = (bf16[2,2,2,16,2304]{4,3,2,1,0:T(8,128)(2,1)}, bf16[2,2,2,16,2304]{4,3,2,1,0:T(8,128)(2,1)}, bf16[2,64,1152]{2,1,0:T(8,128)(2,1)}, bf16[2,64,1152]{2,1,0:T(8,128)(2,1)}, bf16[4,8,2304]{2,1,0:T(8,128)(2,1)}) custom-call(bf16[1,8,2304]{2,1,0:T(8,128)(2,1)} %carry_act.1, bf16[1,8,2304]{2,1,0:T(8,128)(2,1)} %carry_act_tan.1, ...), custom_call_target="tpu_custom_call" | custom-call | tf_op jit(solution)/shard_map/relay/pallas_call | solution.py:550
  56.6 6.3 %curvature.1 = (bf16[1,8,2304]{2,1,0:T(8,128)(2,1)}, bf16[1,8,2304]{2,1,0:T(8,128)(2,1)}, bf16[1,8,2304]{2,1,0:T(8,128)(2,1)}, bf16[1,8,2304]{2,1,0:T(8,128)(2,1...) custom-call(bf16[128,2304]{1,0:T(8,128)(2,1)} %bitcast.4, bf16[128,1152]{1,0:T(8,128)(2,1)} %bitcast.7, ...), custom_call_target="tpu_custom_call" | custom-call | tf_op jit(solution)/shard_map/curvature/pallas_call | solution.py:608
where the time goes:
time: 63.1 us; the launch traced here: 62.9 us
  Pallas kernels  62.3 us (99%)
  between operations  0.65 us (1%)
    pallas_call x1, Pallas kernels, shards(): pl.pallas_call(functools.partial(relay_kernel, sections, n_dp, ticks), ou...  56 us
    pallas_call x1, Pallas kernels, shards(): pl.pallas_call(curvature_kernel, out_shape=(rows_shape,) * 4 + (jax.Shape...  6.3 us

commit v1 on v0

--- a/solution.py
+++ b/solution.py
@@ -52,27 +52,19 @@
 
 
 def over_chunks(size, chunk, body, after=None):
-    count = size // chunk
-
-    def step(index, carry):
-        start = index * chunk if count == 1 else pl.multiple_of(index * chunk, chunk)
-        body(pl.ds(start, chunk))
+    for index in range(size // chunk):
+        body(pl.ds(index * chunk, chunk))
         if after is not None:
             after(index)
+
+
+def turn(source, target, chunk):
+    def step(index, carry):
+        where = pl.ds(pl.multiple_of(index * chunk, chunk), chunk)
+        target[:, where] = source[where, :].T
         return carry
 
-    if count == 1:
-        step(0, 0)
-    else:
-        lax.fori_loop(0, count, step, 0)
-
-
-def once(index, wanted, work):
-    if isinstance(index, int):
-        if index == wanted:
-            work()
-    else:
-        pl.when(index == wanted)(work)
+    lax.fori_loop(0, source.shape[0] // chunk, step, 0)
 
 
 def pair(value, tangent):
@@ -99,10 +91,12 @@
     carry_act, carry_act_tan, carry_adj, carry_adj_tan, fresh_act, loss_cot, stash_act,
     stash_act_tan, norm_gain, up_hbm, down_hbm, up_dir_hbm, down_dir_hbm,
     stash_out, adj_out, hidden_out, delta_out, final_out,
-    up, down, up_dir, down_dir,
+    up, down, up_dir, down_dir, up_turned, down_turned, up_dir_turned, down_dir_turned,
+    gain_row, own_stash,
     left, left_dir, hid, hid_dir, slope, bend, hid_swap, delta, delta_dir, delta_swap,
     adj_dir, stash_all, gathered, outgoing, partial, from_core, to_chip, from_chip,
-    weight_sems, out_sems, core_sems, chip_sems, shift_sems, relay_sems, stash_sems, stash_relay,
+    weight_sems, small_sems, edge_loads, out_sems, core_sems, chip_sems, shift_sems, edge_sems,
+    relay_sems, stash_sems, stash_relay,
 ):
     chips = n_dp // 2
     rows = carry_act.shape[1]
@@ -115,51 +109,138 @@
     section, part = (lax.axis_index("section"), lax.axis_index("dp"))
     chip, core = (part // 2, part % 2)
     other = 1 - core
-    after, before = (lax.rem(section + 1, sections), lax.rem(section + sections - 1, sections))
     partner = (section, chip * 2 + other)
-    gain = norm_gain[...].astype(f32)
+    first, last_one = (section == 0, section == sections - 1)
+    inner_first, inner_last = (section > 0, section < sections - 1)
+    turned = units % 128 == 0
 
     def chip_at(step):
         return lax.rem(chip + step, chips)
 
+    def load_pair(index, value, tangent, target):
+        return [
+            pltpu.make_async_copy(value, target.at[pl.ds(0, rows)], small_sems.at[index, 0]),
+            pltpu.make_async_copy(tangent, target.at[pl.ds(rows, rows)], small_sems.at[index, 1]),
+        ]
+
+    stash_loads = [
+        load_pair(t, stash_act.at[0, t], stash_act_tan.at[0, t], own_stash.at[t])
+        for t in range(ticks)
+    ]
+    adj_loads = load_pair(ticks, carry_adj.at[0], carry_adj_tan.at[0], outgoing.at[1])
+    act_loads = load_pair(ticks + 1, carry_act.at[0], carry_act_tan.at[0], outgoing.at[0])
+    gain_load = pltpu.make_async_copy(norm_gain, gain_row, small_sems.at[ticks + 2, 0])
+
+    def edge_load(lane):
+        source = (fresh_act, loss_cot)[lane % 2]
+        return pltpu.make_async_copy(
+            source.at[lane // 2],
+            gathered.at[lane, core, chip, pl.ds(0, rows)],
+            edge_loads.at[lane],
+        )
+
+    def at_edge(lane):
+        return first if lane % 2 == 0 else last_one
+
+    def inside(lane):
+        return inner_first if lane % 2 == 0 else inner_last
+
+    def sends(lane):
+        return inner_last if lane % 2 == 0 else inner_first
+
+    def call(work, *given):
+        return functools.partial(work, *given)
+
+    def start_all(copies):
+        for copy in copies:
+            copy.start()
+
+    def wait_all(copies):
+        for copy in copies:
+            copy.wait()
+
+    gain_load.start()
+    for tick in range(ticks):
+        start_all(stash_loads[tick])
+    start_all(adj_loads)
+    start_all(act_loads)
+    for lane in range(2 * ticks):
+        pl.when(at_edge(lane))(edge_load(lane).start)
+
+    def weight_loads(number, source, target):
+        cuts = weight_sems.shape[1]
+        part = target.shape[0] // cuts
+        return [
+            pltpu.make_async_copy(
+                source.at[0, pl.ds(cut * part, part)],
+                target.at[pl.ds(cut * part, part)],
+                weight_sems.at[number, cut],
+            )
+            for cut in range(cuts)
+        ]
+
     loads = [
-        pltpu.make_async_copy(source.at[0], target, weight_sems.at[i])
+        weight_loads(i, source, target)
         for i, (source, target) in enumerate(
             ((up_hbm, up), (up_dir_hbm, up_dir), (down_hbm, down), (down_dir_hbm, down_dir))
         )
     ]
-    for load in loads:
-        load.start()
 
     barrier = pltpu.get_barrier_semaphore()
+
+    def greet(where, place):
+        pl.semaphore_signal(barrier, inc=1, device_id=(where, place), device_id_type=MESH)
+
+    def greet_section(where):
+        for step in range(chips):
+            greet(where, chip_at(step) * 2 + core)
+
+    pl.when(inner_last)(lambda: greet_section(section + 1))
+    pl.when(inner_first)(lambda: greet_section(section - 1))
     pl.semaphore_signal(barrier, inc=1, device_id=partner, device_id_type=MESH)
-    for step in range(chips):
-        place = chip_at(step) * 2 + core
-        for where in (after, before):
-            pl.semaphore_signal(barrier, inc=1, device_id=(where, place), device_id_type=MESH)
-        if step:
-            pl.semaphore_signal(barrier, inc=1, device_id=(section, place), device_id_type=MESH)
-
-    def shift_copies(lane):
-        where = after if lane % 2 == 0 else before
+    for step in range(1, chips):
+        greet(section, chip_at(step) * 2 + core)
+
+    def columns(piece):
+        if isinstance(piece, int):
+            return pl.ds(piece * width_chunk, width_chunk)
+        return pl.ds(pl.multiple_of(piece * width_chunk, width_chunk), width_chunk)
+
+    def shift_copies(lane, piece):
+        where = section + 1 if lane % 2 == 0 else section - 1
+        cols = columns(piece)
         return [
             pltpu.make_async_remote_copy(
-                src_ref=outgoing.at[lane],
-                dst_ref=gathered.at[lane, core, chip],
-                send_sem=shift_sems.at[lane, 0, step],
-                recv_sem=shift_sems.at[lane, 1, step],
+                src_ref=outgoing.at[lane, :, cols],
+                dst_ref=gathered.at[lane, core, chip, :, cols],
+                send_sem=shift_sems.at[lane, piece, 0, step],
+                recv_sem=shift_sems.at[lane, piece, 1, step],
                 device_id=(where, chip_at(step) * 2 + core),
                 device_id_type=MESH,
             )
             for step in range(chips)
         ]
 
-    def relay_copy(lane):
+    def edge_copies(lane):
+        return [
+            pltpu.make_async_remote_copy(
+                src_ref=gathered.at[lane, core, chip],
+                dst_ref=gathered.at[lane, core, chip],
+                send_sem=edge_sems.at[lane, 0, step],
+                recv_sem=edge_sems.at[lane, 1, step],
+                device_id=(section, chip_at(step) * 2 + core),
+                device_id_type=MESH,
+            )
+            for step in range(1, chips)
+        ]
+
+    def relay_copy(lane, piece):
+        cols = columns(piece)
         return pltpu.make_async_remote_copy(
-            src_ref=gathered.at[lane, core],
-            dst_ref=gathered.at[lane, core],
-            send_sem=relay_sems.at[lane, 0],
-            recv_sem=relay_sems.at[lane, 1],
+            src_ref=gathered.at[lane, core, :, :, cols],
+            dst_ref=gathered.at[lane, core, :, :, cols],
+            send_sem=relay_sems.at[lane, piece, 0],
+            recv_sem=relay_sems.at[lane, piece, 1],
             device_id=partner,
             device_id_type=MESH,
         )
@@ -192,11 +273,6 @@
             copy.wait_recv()
         stash_relay_copy(tick).start()
 
-    def columns(piece):
-        if isinstance(piece, int):
-            return pl.ds(piece * width_chunk, width_chunk)
-        return pl.ds(pl.multiple_of(piece * width_chunk, width_chunk), width_chunk)
-
     def core_copy(lane, piece):
         return pltpu.make_async_remote_copy(
             src_ref=partial.at[lane, other, :, :, columns(piece)],
@@ -220,24 +296,22 @@
             for step in range(1, chips)
         ]
 
-    def start_all(copies):
-        for copy in copies:
-            copy.start()
-
-    def stage_shift(lane, value, tangent):
-        tick = lane // 2
-        if lane % 2 == 0:
-            ends, entering = (section == sections - 1, fresh_act[tick])
-        else:
-            ends, entering = (section == 0, loss_cot[tick])
-        value = jnp.where(ends, entering.astype(f32), value)
-        tangent = jnp.where(ends, 0.0, tangent)
-        outgoing[lane] = pair(value[None], tangent[None]).astype(bf16)
-
-    def relay(lane):
-        for copy in shift_copies(lane):
-            copy.wait_recv()
-        relay_copy(lane).start()
+    def shift(lane, piece):
+        pl.when(sends(lane))(lambda: start_all(shift_copies(lane, piece)))
+
+    def relay(lane, piece):
+        def from_section():
+            for copy in shift_copies(lane, piece):
+                copy.wait_recv()
+
+        def from_edge():
+            for copy in edge_copies(lane):
+                copy.wait_recv()
+
+        pl.when(inside(lane))(from_section)
+        if piece == 0:
+            pl.when(at_edge(lane))(from_edge)
+        relay_copy(lane, piece).start()
 
     def reduce_in_chip(lane, piece):
         core_copy(lane, piece).wait_recv()
@@ -249,35 +323,20 @@
             to_chip[lane, step - 1, :, cols] = summed.astype(bf16)
         start_all(chip_copies(lane, piece))
 
-    def reduced(lane):
-        for piece in range(pieces):
-            for copy in chip_copies(lane, piece):
-                copy.wait_recv()
-        total = partial[lane, core, chip].astype(f32) + from_core[lane, chip].astype(f32)
+    def reduced(lane, piece):
+        for copy in chip_copies(lane, piece):
+            copy.wait_recv()
+        cols = columns(piece)
+        total = partial[lane, core, chip, :, cols].astype(f32)
+        total = total + from_core[lane, chip, :, cols].astype(f32)
         for step in range(chips - 1):
-            total = total + from_chip[lane, step].astype(f32)
-        return (total[:rows], total[rows:])
+            total = total + from_chip[lane, step, :, cols].astype(f32)
+        return total
 
     def norm_stash(tick):
-        stacked = pair(
-            stash_act[0, tick].astype(f32)[None], stash_act_tan[0, tick].astype(f32)[None]
-        )
-        normed, normed_tan = norm_pair(stacked, gain, rows)
+        gain = gain_row[...].astype(f32)
+        normed, normed_tan = norm_pair(own_stash[tick], gain, rows)
         stash_all[tick, core, chip] = pair(normed, normed_tan).astype(bf16)
-
-    stage_shift(0, carry_act[0].astype(f32), carry_act_tan[0].astype(f32))
-    norm_stash(0)
-    pl.semaphore_wait(barrier, 3 * chips)
-    start_all(shift_copies(0))
-    start_all(stash_copies(0))
-    stage_shift(1, carry_adj[0].astype(f32), carry_adj_tan[0].astype(f32))
-    for tick in range(1, ticks):
-        norm_stash(tick)
-    relay_stash(0)
-    relay(0)
-    start_all(shift_copies(1))
-    for tick in range(1, ticks):
-        start_all(stash_copies(tick))
 
     outs = []
 
@@ -288,7 +347,9 @@
 
     def stage_forward(tick):
         lane = 2 * tick
-        relay_copy(lane).wait_recv()
+        for piece in range(pieces):
+            relay_copy(lane, piece).wait_recv()
+        gain = gain_row[...].astype(f32)
         for block in range(n_dp):
             where = pl.ds(block * 2 * rows, 2 * rows)
             normed, normed_tan = norm_pair(
@@ -307,23 +368,24 @@
             left_dir[where, :] = pair(jnp.zeros_like(value), value).astype(bf16)
         send_out(stash_all.at[tick], stash_out.at[tick])
 
-    def up_products(forward, stash_tick, cols):
-        low = 0 if forward else band
-        high = band if stash_tick is None else 2 * band
-        stacked = matrix_product(left[low:high, :], up[:, cols]) + matrix_product(
-            left_dir[low:high, :], up_dir[:, cols]
-        )
-        if forward:
-            linear, linear_tan = unpair(stacked[:band], rows)
-            value, first, _ = gelu_parts(linear)
-            hid[:, cols] = pair(value, first * linear_tan).astype(bf16)
-            hid_dir[:, cols] = pair(jnp.zeros_like(value), value).astype(bf16)
-        if stash_tick is not None:
-            linear, linear_tan = unpair(stacked[band - low :], rows)
-            value, first, second = gelu_parts(linear)
-            hid_swap[stash_tick, :, cols] = pair(first * linear_tan, value).astype(bf16)
-            slope[stash_tick, :, :, cols] = first
-            bend[stash_tick, :, :, cols] = second * linear_tan
+    def forward_products(cols):
+        stacked = matrix_product(left[:band, :], up[:, cols]) + matrix_product(
+            left_dir[:band, :], up_dir[:, cols]
+        )
+        linear, linear_tan = unpair(stacked, rows)
+        value, slope_now, _ = gelu_parts(linear)
+        hid[:, cols] = pair(value, slope_now * linear_tan).astype(bf16)
+        hid_dir[:, cols] = pair(jnp.zeros_like(value), value).astype(bf16)
+
+    def stash_products(tick, cols):
+        stacked = matrix_product(left[band:, :], up[:, cols]) + matrix_product(
+            left_dir[band:, :], up_dir[:, cols]
+        )
+        linear, linear_tan = unpair(stacked, rows)
+        value, slope_now, second = gelu_parts(linear)
+        hid_swap[tick, :, cols] = pair(slope_now * linear_tan, value).astype(bf16)
+        slope[tick, :, :, cols] = slope_now
+        bend[tick, :, :, cols] = second * linear_tan
 
     def down_products(lane, cols):
         stacked = matrix_product(hid[...], down[:, cols]) + matrix_product(
@@ -333,41 +395,57 @@
 
     def adjoint_products(tick, cols):
         adjoint = gathered[2 * tick + 1].reshape(band, width)
-        stacked = product_last(adjoint, down[cols, :]) + product_last(
-            adj_dir[...], down_dir[cols, :]
-        )
+        if turned and tick:
+            stacked = matrix_product(adjoint, down_turned[:, cols]) + matrix_product(
+                adj_dir[...], down_dir_turned[:, cols]
+            )
+        elif turned:
+            stacked = matrix_product(adjoint, down_turned[:, cols]) + product_last(
+                adj_dir[...], down_dir[cols, :]
+            )
+        else:
+            stacked = product_last(adjoint, down[cols, :]) + product_last(
+                adj_dir[...], down_dir[cols, :]
+            )
         upstream, upstream_tan = unpair(stacked, rows)
-        first, second_tan = (slope[tick, :, :, cols], bend[tick, :, :, cols])
-        value = upstream * first
-        tangent = upstream_tan * first + upstream * second_tan
+        slope_now, second_tan = (slope[tick, :, :, cols], bend[tick, :, :, cols])
+        value = upstream * slope_now
+        tangent = upstream_tan * slope_now + upstream * second_tan
         delta[:, cols] = pair(value, tangent).astype(bf16)
         delta_dir[:, cols] = pair(jnp.zeros_like(value), value).astype(bf16)
         delta_swap[tick, :, cols] = pair(tangent, value).astype(bf16)
 
     def back_products(lane, cols):
-        stacked = product_last(delta[...], up[cols, :]) + product_last(
-            delta_dir[...], up_dir[cols, :]
-        )
+        if turned:
+            stacked = matrix_product(delta[...], up_turned[:, cols]) + matrix_product(
+                delta_dir[...], up_dir_turned[:, cols]
+            )
+        else:
+            stacked = product_last(delta[...], up[cols, :]) + product_last(
+                delta_dir[...], up_dir[cols, :]
+            )
         partial[lane, :, :, :, cols] = stacked.astype(bf16).reshape(2, chips, 2 * rows, -1)
 
     def finish_forward(tick):
         lane = 2 * tick
-        value, tangent = reduced(lane)
-        own = gathered[lane, core, chip].astype(f32)
-        value, tangent = (own[:rows] + value, own[rows:] + tangent)
-        if tick + 1 < ticks:
-            stage_shift(lane + 2, value, tangent)
-            start_all(shift_copies(lane + 2))
-        else:
-            final_out[0] = value.astype(bf16)
-            final_out[1] = tangent.astype(bf16)
+        for piece in range(pieces):
+            cols = columns(piece)
+            total = reduced(lane, piece) + gathered[lane, core, chip, :, cols].astype(f32)
+            if tick + 1 < ticks:
+                outgoing[lane + 2, :, cols] = total.astype(bf16)
+                shift(lane + 2, piece)
+            else:
+                final_out[0, :, cols] = total[:rows].astype(bf16)
+                final_out[1, :, cols] = total[rows:].astype(bf16)
 
     def finish_backward(tick):
         lane = 2 * tick + 1
-        summed, summed_tan = reduced(lane)
+        total = jnp.concatenate([reduced(lane, piece) for piece in range(pieces)], axis=-1)
+        summed, summed_tan = (total[:rows], total[rows:])
+        gain = gain_row[...].astype(f32)
         arriving = gathered[lane, core, chip].astype(f32)
-        values = stash_act[0, tick].astype(f32)
-        values_tan = stash_act_tan[0, tick].astype(f32)
+        both = own_stash[tick].astype(f32)
+        values, values_tan = (both[:rows], both[rows:])
         inverse = lax.rsqrt(jnp.mean(values * values, axis=-1, keepdims=True) + norm_eps)
         cube = inverse * inverse * inverse
         inverse_tan = -cube * jnp.mean(values * values_tan, axis=-1, keepdims=True)
@@ -386,21 +464,20 @@
             - cube * values * moment_tan
         )
         if tick + 1 < ticks:
-            stage_shift(lane + 2, value, tangent)
-            start_all(shift_copies(lane + 2))
+            outgoing[lane + 2] = pair(value[None], tangent[None]).astype(bf16)
+            for piece in range(pieces):
+                shift(lane + 2, piece)
         else:
             final_out[2] = value.astype(bf16)
             final_out[3] = tangent.astype(bf16)
 
-    def call(work, *given):
-        return functools.partial(work, *given)
-
     def start_piece(lane, piece):
         core_copy(lane, piece).start()
 
     def stage_adjoint(tick):
         lane = 2 * tick + 1
-        relay_copy(lane).wait_recv()
+        for piece in range(pieces):
+            relay_copy(lane, piece).wait_recv()
         for block in range(n_dp):
             value = unpair(gathered[lane, block // chips, block % chips], rows)[0]
             adj_dir[pl.ds(block * 2 * rows, 2 * rows), :] = pair(
@@ -408,58 +485,131 @@
             ).astype(bf16)
         send_out(gathered.at[lane], adj_out.at[tick])
 
-    stage_forward(0)
+    def enter_edge(lane):
+        def load_rows():
+            edge_load(lane).wait()
+            gathered[lane, core, chip, rows:, :] = jnp.zeros((rows, width), bf16)
+
+        pl.when(at_edge(lane))(load_rows)
+
+    def send_edge(lane):
+        pl.when(at_edge(lane))(lambda: start_all(edge_copies(lane)))
+
+    gain_load.wait()
+    for tick in range(ticks):
+        wait_all(stash_loads[tick])
+    wait_all(adj_loads)
+    wait_all(act_loads)
+    for lane in range(2 * ticks):
+        enter_edge(lane)
+    for load in loads:
+        start_all(load)
+    norm_stash(0)
+    sides = inner_first.astype(jnp.int32) + inner_last.astype(jnp.int32)
+    pl.semaphore_wait(barrier, chips + chips * sides)
+    start_all(stash_copies(0))
+
+    def first_shift(lane):
+        copies = [shift_copies(lane, piece) for piece in range(pieces)]
+        for step in range(chips):
+            for piece in range(pieces):
+                copies[piece][step].start()
+
+    pl.when(sends(1))(call(first_shift, 1))
+    pl.when(sends(0))(call(first_shift, 0))
+    for lane in (1, 0):
+        send_edge(lane)
+    for tick in range(1, ticks):
+        norm_stash(tick)
+
+    def turn_part(source, target, index):
+        where = pl.ds(index * unit_chunk, unit_chunk)
+        target[:, where] = source[where, :].T
+
+    def all_pieces(work, *given):
+        for piece in range(pieces):
+            work(*given, piece)
+
+    def enter_weights(number, source, target):
+        part = source.shape[0] // len(loads[number])
+        for cut, load in enumerate(loads[number]):
+            load.wait()
+            if turned:
+                where = pl.ds(cut * part, part)
+                target[:, where] = source[where, :].T
+
+    enter_weights(0, up, up_turned)
+    relay_stash(0)
+    enter_weights(1, up_dir, up_dir_turned)
     stage_stash(0)
-    loads[0].wait()
-    loads[1].wait()
-    last = pieces - 1
+    wait_all(loads[2])
+
+    def beside_stash(index):
+        if turned:
+            turn_part(down, down_turned, index)
+
+    over_chunks(units, unit_chunk, call(stash_products, 0), beside_stash)
+    send_out(hid_swap.at[0], hidden_out.at[0])
+    for tick in range(1, ticks):
+        start_all(stash_copies(tick))
+        send_edge(2 * tick + 1)
+        send_edge(2 * tick)
+    all_pieces(relay, 1)
+    all_pieces(relay, 0)
     for tick in range(ticks):
         ahead, behind = (2 * tick, 2 * tick + 1)
+        stage_adjoint(tick)
+        if tick == 0:
+            wait_all(loads[3])
+        over_chunks(units, unit_chunk, call(adjoint_products, tick))
         if tick:
-            stage_forward(tick)
-        over_chunks(units, unit_chunk, call(up_products, True, None if tick else 0))
-        if tick == 0:
-            send_out(hid_swap.at[0], hidden_out.at[0])
-            loads[2].wait()
-            loads[3].wait()
-        over_chunks(width, width_chunk, call(down_products, ahead), call(start_piece, ahead))
-        relay(behind)
-        stage_adjoint(tick)
-
-        def reduce_pieces(index):
-            def all_pieces():
-                for piece in range(pieces):
-                    reduce_in_chip(ahead, piece)
-
-            once(index, 0, all_pieces)
-
-        over_chunks(units, unit_chunk, call(adjoint_products, tick), reduce_pieces)
+            all_pieces(relay, ahead)
+        over_chunks(width, width_chunk, call(back_products, behind))
+        all_pieces(start_piece, behind)
         send_out(delta_swap.at[tick], delta_out.at[tick])
-        finish_forward(tick)
+        stage_forward(tick)
+
+        def beside_forward(index, tick=tick, behind=behind):
+            if turned and tick == 0:
+                turn_part(down_dir, down_dir_turned, index)
+            if index == 0:
+                all_pieces(reduce_in_chip, behind)
+
+        over_chunks(units, unit_chunk, forward_products, beside_forward)
+        over_chunks(width, width_chunk, call(down_products, ahead))
+        all_pieces(start_piece, ahead)
+        finish_backward(tick)
         if tick + 1 < ticks:
             relay_stash(tick + 1)
-
-        def pass_piece(index):
-            start_piece(behind, index)
-            for piece in range(1, pieces):
-                once(index, piece, call(reduce_in_chip, behind, piece - 1))
-
-        over_chunks(width, width_chunk, call(back_products, behind), pass_piece)
-        if tick + 1 < ticks:
-            reduce_in_chip(behind, last)
             stage_stash(tick + 1)
-            over_chunks(units, unit_chunk, call(up_products, False, tick + 1))
+
+            def beside_next(index, ahead=ahead):
+                if index == 0:
+                    all_pieces(reduce_in_chip, ahead)
+
+            over_chunks(units, unit_chunk, call(stash_products, tick + 1), beside_next)
             send_out(hid_swap.at[tick + 1], hidden_out.at[tick + 1])
-            relay(ahead + 2)
+            finish_forward(tick)
+            all_pieces(relay, behind + 2)
         else:
-            reduce_in_chip(behind, last)
-        finish_backward(tick)
+            all_pieces(reduce_in_chip, ahead)
+            finish_forward(tick)
 
     for lane in range(2 * ticks):
-        for copy in shift_copies(lane):
-            copy.wait_send()
-        relay_copy(lane).wait_send()
+
+        def sent(lane=lane):
+            for piece in range(pieces):
+                for copy in shift_copies(lane, piece):
+                    copy.wait_send()
+
+        def sent_edge(lane=lane):
+            for copy in edge_copies(lane):
+                copy.wait_send()
+
+        pl.when(sends(lane))(sent)
+        pl.when(at_edge(lane))(sent_edge)
         for piece in range(pieces):
+            relay_copy(lane, piece).wait_send()
             core_copy(lane, piece).wait_send()
             for copy in chip_copies(lane, piece):
                 copy.wait_send()
@@ -547,6 +697,8 @@
         pl.BlockSpec(memory_space=pl.ANY),
     )
     block = (2 * rows, width)
+    turned = units % 128 == 0
+    up_turn, down_turn = ((units, width), (width, units)) if turned else ((16, 128), (16, 128))
     stash_out, adj_out, hidden_out, delta_out, final_out = pl.pallas_call(
         functools.partial(relay_kernel, sections, n_dp, ticks),
         out_shape=(
@@ -556,13 +708,19 @@
             jax.ShapeDtypeStruct((ticks, band, units), bf16),
             jax.ShapeDtypeStruct((4, rows, width), bf16),
         ),
-        in_specs=[vmem] * 9 + [anywhere] * 4,
+        in_specs=[anywhere] * 13,
         out_specs=(anywhere,) * 4 + (vmem,),
         scratch_shapes=[
             pltpu.VMEM((width, units), bf16),
             pltpu.VMEM((units, width), bf16),
             pltpu.VMEM((width, units), bf16),
             pltpu.VMEM((units, width), bf16),
+            pltpu.VMEM(up_turn, bf16),
+            pltpu.VMEM(down_turn, bf16),
+            pltpu.VMEM(up_turn, bf16),
+            pltpu.VMEM(down_turn, bf16),
+            pltpu.VMEM((1, width), bf16),
+            pltpu.VMEM((ticks,) + block, bf16),
             pltpu.VMEM((tall, width), bf16),
             pltpu.VMEM((tall, width), bf16),
             pltpu.VMEM((band, units), bf16),
@@ -581,12 +739,15 @@
             pltpu.VMEM((lanes, chips) + block, bf16),
             pltpu.VMEM((lanes, chips - 1) + block, bf16),
             pltpu.VMEM((lanes, chips - 1) + block, bf16),
-            pltpu.SemaphoreType.DMA((4,)),
+            pltpu.SemaphoreType.DMA((4, 3)),
+            pltpu.SemaphoreType.DMA((ticks + 3, 2)),
+            pltpu.SemaphoreType.DMA((lanes,)),
             pltpu.SemaphoreType.DMA((4 * ticks,)),
             pltpu.SemaphoreType.DMA((lanes, pieces, 2)),
             pltpu.SemaphoreType.DMA((lanes, pieces, 2, chips - 1)),
+            pltpu.SemaphoreType.DMA((lanes, pieces, 2, chips)),
             pltpu.SemaphoreType.DMA((lanes, 2, chips)),
-            pltpu.SemaphoreType.DMA((lanes, 2)),
+            pltpu.SemaphoreType.DMA((lanes, pieces, 2)),
             pltpu.SemaphoreType.DMA((ticks, 2, chips)),
             pltpu.SemaphoreType.DMA((ticks, 2)),
         ],

time: 63.1 us -> 52.2 us (0.83)
  Pallas kernels: 62.3 us -> 51.2 us
    pallas_call x1, Pallas kernels: 56 us -> 44.9 us  [shards(): pl.pallas_call(functools.partial(relay_kernel, sections, n_dp, ticks), ou...]
where the time goes in v1:
time: 52.2 us; the launch traced here: 52 us
  Pallas kernels  51.2 us (98%)
  between operations  0.81 us (2%)
    pallas_call x1, Pallas kernels, shards(): pl.pallas_call(functools.partial(relay_kernel, sections, n_dp, ticks), ou...  44.9 us
    pallas_call x1, Pallas kernels, shards(): pl.pallas_call(curvature_kernel, out_shape=(rows_shape,) * 4 + (jax.Shape...  6.3 us

profile of v1, /device:TPU:0, one launch (start us, length us, event | category | flops | bytes accessed | tf_op | source)
XLA Modules:
  0.0 52.0 jit_solution(14774232526922838894)
XLA Ops:
  0.6 44.9 %relay.1 = (bf16[2,2,2,16,2304]{4,3,2,1,0:T(8,128)(2,1)}, bf16[2,2,2,16,2304]{4,3,2,1,0:T(8,128)(2,1)}, bf16[2,64,1152]{2,1,0:T(8,128)(2,1)}, bf16[2,64,1152]{2,1,0:T(8,128)(2,1)}, bf16[4,8,2304]{2,1,0:T(8,128)(2,1)}) custom-call(bf16[1,8,2304]{2,1,0:T(8,128)(2,1)} %carry_act.1, bf16[1,8,2304]{2,1,0:T(8,128)(2,1)} %carry_act_tan.1, ...), custom_call_target="tpu_custom_call" | custom-call | tf_op jit(solution)/shard_map/relay/pallas_call | solution.py:702
  45.5 6.3 %curvature.1 = (bf16[1,8,2304]{2,1,0:T(8,128)(2,1)}, bf16[1,8,2304]{2,1,0:T(8,128)(2,1)}, bf16[1,8,2304]{2,1,0:T(8,128)(2,1)}, bf16[1,8,2304]{2,1,0:T(8,128)(2,1...) custom-call(bf16[128,2304]{1,0:T(8,128)(2,1)} %bitcast.4, bf16[128,1152]{1,0:T(8,128)(2,1)} %bitcast.7, ...), custom_call_target="tpu_custom_call" | custom-call | tf_op jit(solution)/shard_map/curvature/pallas_call | solution.py:769

commit v2 on v1

--- a/solution.py
+++ b/solution.py
@@ -90,12 +90,12 @@
     sections, n_dp, ticks,
     carry_act, carry_act_tan, carry_adj, carry_adj_tan, fresh_act, loss_cot, stash_act,
     stash_act_tan, norm_gain, up_hbm, down_hbm, up_dir_hbm, down_dir_hbm,
-    stash_out, adj_out, hidden_out, delta_out, final_out,
-    up, down, up_dir, down_dir, up_turned, down_turned, up_dir_turned, down_dir_turned,
+    final_out, curve_up, curve_down,
+    up, down, up_dir, down_dir, up_dir_turned, down_dir_turned,
     gain_row, own_stash,
     left, left_dir, hid, hid_dir, slope, bend, hid_swap, delta, delta_dir, delta_swap,
     adj_dir, stash_all, gathered, outgoing, partial, from_core, to_chip, from_chip,
-    weight_sems, small_sems, edge_loads, out_sems, core_sems, chip_sems, shift_sems, edge_sems,
+    weight_sems, small_sems, edge_loads, core_sems, chip_sems, shift_sems, edge_sems,
     relay_sems, stash_sems, stash_relay,
 ):
     chips = n_dp // 2
@@ -113,6 +113,7 @@
     first, last_one = (section == 0, section == sections - 1)
     inner_first, inner_last = (section > 0, section < sections - 1)
     turned = units % 128 == 0
+    up_turned, down_turned = (curve_down, curve_up)
 
     def chip_at(step):
         return lax.rem(chip + step, chips)
@@ -338,13 +339,6 @@
         normed, normed_tan = norm_pair(own_stash[tick], gain, rows)
         stash_all[tick, core, chip] = pair(normed, normed_tan).astype(bf16)
 
-    outs = []
-
-    def send_out(source, target):
-        copy = pltpu.make_async_copy(source, target, out_sems.at[len(outs)])
-        copy.start()
-        outs.append(copy)
-
     def stage_forward(tick):
         lane = 2 * tick
         for piece in range(pieces):
@@ -366,7 +360,6 @@
             left[where, :] = stacked
             value = unpair(stacked, rows)[0]
             left_dir[where, :] = pair(jnp.zeros_like(value), value).astype(bf16)
-        send_out(stash_all.at[tick], stash_out.at[tick])
 
     def forward_products(cols):
         stacked = matrix_product(left[:band, :], up[:, cols]) + matrix_product(
@@ -483,7 +476,6 @@
             adj_dir[pl.ds(block * 2 * rows, 2 * rows), :] = pair(
                 jnp.zeros_like(value), value
             ).astype(bf16)
-        send_out(gathered.at[lane], adj_out.at[tick])
 
     def enter_edge(lane):
         def load_rows():
@@ -516,11 +508,28 @@
                 copies[piece][step].start()
 
     pl.when(sends(1))(call(first_shift, 1))
-    pl.when(sends(0))(call(first_shift, 0))
-    for lane in (1, 0):
-        send_edge(lane)
+    send_edge(1)
     for tick in range(1, ticks):
         norm_stash(tick)
+
+    def curvature():
+        deep = ticks * band
+
+        adjoints = jnp.concatenate(
+            [gathered[2 * tick + 1].reshape(band, width) for tick in range(ticks)], axis=0
+        )
+        deltas = delta_swap[...].reshape(deep, units)
+        for index in range(max(pieces, units // unit_chunk)):
+            if index < pieces:
+                where = columns(index)
+                curve_up[where, :] = product_first(
+                    stash_all[:, :, :, :, where].reshape(deep, width_chunk), deltas
+                ).astype(bf16)
+            if index < units // unit_chunk:
+                where = pl.ds(index * unit_chunk, unit_chunk)
+                curve_down[where, :] = product_first(
+                    hid_swap[:, :, where].reshape(deep, unit_chunk), adjoints
+                ).astype(bf16)
 
     def turn_part(source, target, index):
         where = pl.ds(index * unit_chunk, unit_chunk)
@@ -542,6 +551,8 @@
     relay_stash(0)
     enter_weights(1, up_dir, up_dir_turned)
     stage_stash(0)
+    pl.when(sends(0))(call(first_shift, 0))
+    send_edge(0)
     wait_all(loads[2])
 
     def beside_stash(index):
@@ -549,24 +560,22 @@
             turn_part(down, down_turned, index)
 
     over_chunks(units, unit_chunk, call(stash_products, 0), beside_stash)
-    send_out(hid_swap.at[0], hidden_out.at[0])
     for tick in range(1, ticks):
         start_all(stash_copies(tick))
         send_edge(2 * tick + 1)
         send_edge(2 * tick)
     all_pieces(relay, 1)
-    all_pieces(relay, 0)
     for tick in range(ticks):
         ahead, behind = (2 * tick, 2 * tick + 1)
         stage_adjoint(tick)
         if tick == 0:
             wait_all(loads[3])
         over_chunks(units, unit_chunk, call(adjoint_products, tick))
-        if tick:
-            all_pieces(relay, ahead)
+        all_pieces(relay, ahead)
         over_chunks(width, width_chunk, call(back_products, behind))
         all_pieces(start_piece, behind)
-        send_out(delta_swap.at[tick], delta_out.at[tick])
+        if tick + 1 < ticks:
+            relay_stash(tick + 1)
         stage_forward(tick)
 
         def beside_forward(index, tick=tick, behind=behind):
@@ -580,7 +589,6 @@
         all_pieces(start_piece, ahead)
         finish_backward(tick)
         if tick + 1 < ticks:
-            relay_stash(tick + 1)
             stage_stash(tick + 1)
 
             def beside_next(index, ahead=ahead):
@@ -588,11 +596,11 @@
                     all_pieces(reduce_in_chip, ahead)
 
             over_chunks(units, unit_chunk, call(stash_products, tick + 1), beside_next)
-            send_out(hid_swap.at[tick + 1], hidden_out.at[tick + 1])
             finish_forward(tick)
             all_pieces(relay, behind + 2)
         else:
             all_pieces(reduce_in_chip, ahead)
+            curvature()
             finish_forward(tick)
 
     for lane in range(2 * ticks):
@@ -617,66 +625,27 @@
         for copy in stash_copies(tick):
             copy.wait_send()
         stash_relay_copy(tick).wait_send()
-    for copy in outs:
-        copy.wait()
-
-
-def curvature_kernel(
-    stash_hbm, delta_hbm, hidden_hbm, adj_hbm, final_hbm,
-    act, act_tan, adj_new, adj_new_tan, up_hbm, down_hbm,
-    stash_sw, delta_sw, hidden_sw, adj, final, up_out, down_out, in_sems, row_sems, up_sems, down_sems,
+
+
+def deliver_kernel(
+    final, curve_up, curve_down, act, act_tan, adj_new, adj_new_tan, up_hbm, down_hbm, row_sems, part_sems
 ):
-    sources = (stash_hbm, delta_hbm, hidden_hbm, adj_hbm, final_hbm)
-    targets = (stash_sw, delta_sw, hidden_sw, adj, final)
-    loads = [
-        pltpu.make_async_copy(source, target, in_sems.at[i])
-        for i, (source, target) in enumerate(zip(sources, targets))
-    ]
-    for load in loads:
-        load.start()
-    for load in loads:
-        load.wait()
-    row_copies = [
-        pltpu.make_async_copy(final.at[i], target.at[0], row_sems.at[i])
-        for i, target in enumerate((act, act_tan, adj_new, adj_new_tan))
-    ]
-    for copy in row_copies:
+    copies = []
+    for number, (source, target) in enumerate(((curve_up, up_hbm), (curve_down, down_hbm))):
+        cuts = part_sems.shape[1]
+        part = source.shape[0] // cuts
+        for cut in range(cuts):
+            where = pl.ds(cut * part, part)
+            copies.append(
+                pltpu.make_async_copy(
+                    source.at[where], target.at[0, where], part_sems.at[number, cut]
+                )
+            )
+    for i, target in enumerate((act, act_tan, adj_new, adj_new_tan)):
+        copies.append(pltpu.make_async_copy(final.at[i], target.at[0], row_sems.at[i]))
+    for copy in copies:
         copy.start()
-
-    def product(left, right, out, target, sems):
-        chunk = out.shape[0] // sems.shape[0]
-
-        def part(piece):
-            where = pl.ds(piece * chunk, chunk)
-            if not isinstance(piece, int):
-                where = pl.ds(pl.multiple_of(piece * chunk, chunk), chunk)
-            out[where, :] = product_first(left[:, where], right[...]).astype(bf16)
-            copy = pltpu.make_async_copy(out.at[where, :], target.at[0, where, :], sems.at[piece])
-            copy.start()
-
-        return part
-
-    up_part = product(stash_sw, delta_sw, up_out, up_hbm, up_sems)
-    down_part = product(hidden_sw, adj, down_out, down_hbm, down_sems)
-    if up_sems.shape[0] == down_sems.shape[0] > 1:
-
-        def step(piece, carry):
-            up_part(piece)
-            down_part(piece)
-            return carry
-
-        lax.fori_loop(0, up_sems.shape[0], step, 0)
-    else:
-        for piece in range(up_sems.shape[0]):
-            up_part(piece)
-        for piece in range(down_sems.shape[0]):
-            down_part(piece)
-    for out, target, sems in ((up_out, up_hbm, up_sems), (down_out, down_hbm, down_sems)):
-        chunk = out.shape[0] // sems.shape[0]
-        for piece in range(sems.shape[0]):
-            where = pl.ds(piece * chunk, chunk)
-            pltpu.make_async_copy(out.at[where, :], target.at[0, where, :], sems.at[piece]).wait()
-    for copy in row_copies:
+    for copy in copies:
         copy.wait()
 
 
@@ -699,24 +668,20 @@
     block = (2 * rows, width)
     turned = units % 128 == 0
     up_turn, down_turn = ((units, width), (width, units)) if turned else ((16, 128), (16, 128))
-    stash_out, adj_out, hidden_out, delta_out, final_out = pl.pallas_call(
+    final_out, curve_up, curve_down = pl.pallas_call(
         functools.partial(relay_kernel, sections, n_dp, ticks),
         out_shape=(
-            jax.ShapeDtypeStruct((ticks, 2, chips) + block, bf16),
-            jax.ShapeDtypeStruct((ticks, 2, chips) + block, bf16),
-            jax.ShapeDtypeStruct((ticks, band, units), bf16),
-            jax.ShapeDtypeStruct((ticks, band, units), bf16),
-            jax.ShapeDtypeStruct((4, rows, width), bf16),
+            pltpu.VMEM((4, rows, width), bf16),
+            pltpu.VMEM((width, units), bf16),
+            pltpu.VMEM((units, width), bf16),
         ),
         in_specs=[anywhere] * 13,
-        out_specs=(anywhere,) * 4 + (vmem,),
+        out_specs=(vmem,) * 3,
         scratch_shapes=[
             pltpu.VMEM((width, units), bf16),
             pltpu.VMEM((units, width), bf16),
             pltpu.VMEM((width, units), bf16),
             pltpu.VMEM((units, width), bf16),
-            pltpu.VMEM(up_turn, bf16),
-            pltpu.VMEM(down_turn, bf16),
             pltpu.VMEM(up_turn, bf16),
             pltpu.VMEM(down_turn, bf16),
             pltpu.VMEM((1, width), bf16),
@@ -742,7 +707,6 @@
             pltpu.SemaphoreType.DMA((4, 3)),
             pltpu.SemaphoreType.DMA((ticks + 3, 2)),
             pltpu.SemaphoreType.DMA((lanes,)),
-            pltpu.SemaphoreType.DMA((4 * ticks,)),
             pltpu.SemaphoreType.DMA((lanes, pieces, 2)),
             pltpu.SemaphoreType.DMA((lanes, pieces, 2, chips - 1)),
             pltpu.SemaphoreType.DMA((lanes, pieces, 2, chips)),
@@ -752,45 +716,31 @@
             pltpu.SemaphoreType.DMA((ticks, 2)),
         ],
         compiler_params=pltpu.CompilerParams(
-            collective_id=0, has_side_effects=True, vmem_limit_bytes=60 * 1024 * 1024
+            collective_id=0, has_side_effects=True, vmem_limit_bytes=46 * 1024 * 1024
         ),
         name="relay",
     )(
         carry_act, carry_act_tan, carry_adj, carry_adj_tan, fresh_act, loss_cot, stash_act,
         stash_act_tan, norm_gain, up_weight, down_weight, up_dir, down_dir,
     )
-    deep = band * ticks
-    stash_sw = stash_out.reshape(deep, width)
-    delta_sw = delta_out.reshape(deep, units)
-    hidden_sw = hidden_out.reshape(deep, units)
-    adj_flat = adj_out.reshape(deep, width)
     rows_shape = jax.ShapeDtypeStruct((1, rows, width), bf16)
     return tuple(
         pl.pallas_call(
-            curvature_kernel,
+            deliver_kernel,
             out_shape=(rows_shape,) * 4
             + (
                 jax.ShapeDtypeStruct((1, width, units), bf16),
                 jax.ShapeDtypeStruct((1, units, width), bf16),
             ),
-            in_specs=[anywhere] * 5,
+            in_specs=[vmem] * 3,
             out_specs=(anywhere,) * 6,
             scratch_shapes=[
-                pltpu.VMEM((deep, width), bf16),
-                pltpu.VMEM((deep, units), bf16),
-                pltpu.VMEM((deep, units), bf16),
-                pltpu.VMEM((deep, width), bf16),
-                pltpu.VMEM((4, rows, width), bf16),
-                pltpu.VMEM((width, units), bf16),
-                pltpu.VMEM((units, width), bf16),
-                pltpu.SemaphoreType.DMA((5,)),
                 pltpu.SemaphoreType.DMA((4,)),
-                pltpu.SemaphoreType.DMA((width // lane_chunk(width, 768),)),
-                pltpu.SemaphoreType.DMA((units // lane_chunk(units, 384),)),
+                pltpu.SemaphoreType.DMA((2, 3)),
             ],
-            compiler_params=pltpu.CompilerParams(vmem_limit_bytes=60 * 1024 * 1024),
-            name="curvature",
-        )(stash_sw, delta_sw, hidden_sw, adj_flat, final_out)
+            compiler_params=pltpu.CompilerParams(vmem_limit_bytes=1024 * 1024),
+            name="deliver",
+        )(final_out, curve_up, curve_down)
     )
 
 

time: 52.2 us -> 49 us (0.939)
  Pallas kernels: 51.2 us -> 47.9 us
    pallas_call x1, Pallas kernels: 6.3 us -> 4.15 us  [shards(): pl.pallas_call(deliver_kernel, out_shape=(rows_shape,) * 4 + (jax.ShapeDt...]
    pallas_call x1, Pallas kernels: 44.9 us -> 43.8 us  [shards(): pl.pallas_call(functools.partial(relay_kernel, sections, n_dp, ticks), ou...]
where the time goes in v2:
time: 49 us; the launch traced here: 48.7 us
  Pallas kernels  47.9 us (98%)
  between operations  0.81 us (2%)
    pallas_call x1, Pallas kernels, shards(): pl.pallas_call(functools.partial(relay_kernel, sections, n_dp, ticks), ou...  43.8 us
    pallas_call x1, Pallas kernels, shards(): pl.pallas_call(deliver_kernel, out_shape=(rows_shape,) * 4 + (jax.ShapeDt...  4.15 us

profile of v2, /device:TPU:0, one launch (start us, length us, event | category | flops | bytes accessed | tf_op | source)
XLA Modules:
  0.0 48.7 jit_solution(3006642314075150616)
XLA Ops:
  0.6 43.8 %relay.1 = (bf16[4,8,2304]{2,1,0:T(8,128)(2,1)S(1)}, bf16[2304,1152]{1,0:T(8,128)(2,1)S(1)}, bf16[1152,2304]{1,0:T(8,128)(2,1)S(1)}) custom-call(bf16[1,8,2304]{2,1,0:T(8,128)(2,1)} %carry_act.1, bf16[1,8,2304]{2,1,0:T(8,128)(2,1)} %carry_act_tan.1, bf16[1,8,2304]{2,1,0:T(8,128)(2,1)} %carry_adj.1, bf16[1,8,2304]{2,1,0:T(8,128)(2,1)} %carry_adj_tan.1, ...), custom_call_target="tpu_custom_call" | custom-call | tf_op jit(solution)/shard_map/relay/pallas_call | solution.py:671
  44.4 4.1 %deliver.1 = (bf16[1,8,2304]{2,1,0:T(8,128)(2,1)}, bf16[1,8,2304]{2,1,0:T(8,128)(2,1)}, bf16[1,8,2304]{2,1,0:T(8,128)(2,1)}, bf16[1,8,2304]{2,1,0:T(8,128)(2,1)}...) custom-call(bf16[4,8,2304]{2,1,0:T(8,128)(2,1)S(1)} %get-tuple-element.9.final, ...), custom_call_target="tpu_custom_call" | custom-call | tf_op jit(solution)/shard_map/deliver/pallas_call | solution.py:728

commit v3 on v2

--- a/solution.py
+++ b/solution.py
@@ -548,23 +548,26 @@
                 target[:, where] = source[where, :].T
 
     enter_weights(0, up, up_turned)
+    enter_weights(1, up_dir, up_dir_turned)
     relay_stash(0)
-    enter_weights(1, up_dir, up_dir_turned)
     stage_stash(0)
     pl.when(sends(0))(call(first_shift, 0))
     send_edge(0)
     wait_all(loads[2])
 
+    parts = units // unit_chunk
+
     def beside_stash(index):
         if turned:
             turn_part(down, down_turned, index)
+        if index == max(parts - 2, 0):
+            all_pieces(relay, 1)
 
     over_chunks(units, unit_chunk, call(stash_products, 0), beside_stash)
     for tick in range(1, ticks):
         start_all(stash_copies(tick))
         send_edge(2 * tick + 1)
         send_edge(2 * tick)
-    all_pieces(relay, 1)
     for tick in range(ticks):
         ahead, behind = (2 * tick, 2 * tick + 1)
         stage_adjoint(tick)
@@ -572,27 +575,28 @@
             wait_all(loads[3])
         over_chunks(units, unit_chunk, call(adjoint_products, tick))
         all_pieces(relay, ahead)
-        over_chunks(width, width_chunk, call(back_products, behind))
+        over_chunks(width, width, call(back_products, behind))
         all_pieces(start_piece, behind)
         if tick + 1 < ticks:
             relay_stash(tick + 1)
         stage_forward(tick)
 
         def beside_forward(index, tick=tick, behind=behind):
+            reduce_at = 0 if tick + 1 < ticks else min(1, parts - 1)
             if turned and tick == 0:
                 turn_part(down_dir, down_dir_turned, index)
-            if index == 0:
+            if index == reduce_at:
                 all_pieces(reduce_in_chip, behind)
 
         over_chunks(units, unit_chunk, forward_products, beside_forward)
-        over_chunks(width, width_chunk, call(down_products, ahead))
+        over_chunks(width, width, call(down_products, ahead))
         all_pieces(start_piece, ahead)
-        finish_backward(tick)
         if tick + 1 < ticks:
+            finish_backward(tick)
             stage_stash(tick + 1)
 
             def beside_next(index, ahead=ahead):
-                if index == 0:
+                if index == min(1, parts - 1):
                     all_pieces(reduce_in_chip, ahead)
 
             over_chunks(units, unit_chunk, call(stash_products, tick + 1), beside_next)
@@ -600,6 +604,7 @@
             all_pieces(relay, behind + 2)
         else:
             all_pieces(reduce_in_chip, ahead)
+            finish_backward(tick)
             curvature()
             finish_forward(tick)
 

time: 49 us -> 47.9 us (0.978)
  Pallas kernels: 47.9 us -> 46.8 us
    pallas_call x1, Pallas kernels: 43.8 us -> 42.7 us  [shards(): pl.pallas_call(functools.partial(relay_kernel, sections, n_dp, ticks), ou...]
where the time goes in v3:
time: 47.9 us; the launch traced here: 47.6 us
  Pallas kernels  46.8 us (98%)
  between operations  0.81 us (2%)
    pallas_call x1, Pallas kernels, shards(): pl.pallas_call(functools.partial(relay_kernel, sections, n_dp, ticks), ou...  42.7 us
    pallas_call x1, Pallas kernels, shards(): pl.pallas_call(deliver_kernel, out_shape=(rows_shape,) * 4 + (jax.ShapeDt...  4.15 us

profile of v3, /device:TPU:0, one launch (start us, length us, event | category | flops | bytes accessed | tf_op | source)
XLA Modules:
  0.0 47.6 jit_solution(443205644615965089)
XLA Ops:
  0.6 42.7 %relay.1 = (bf16[4,8,2304]{2,1,0:T(8,128)(2,1)S(1)}, bf16[2304,1152]{1,0:T(8,128)(2,1)S(1)}, bf16[1152,2304]{1,0:T(8,128)(2,1)S(1)}) custom-call(bf16[1,8,2304]{2,1,0:T(8,128)(2,1)} %carry_act.1, bf16[1,8,2304]{2,1,0:T(8,128)(2,1)} %carry_act_tan.1, bf16[1,8,2304]{2,1,0:T(8,128)(2,1)} %carry_adj.1, bf16[1,8,2304]{2,1,0:T(8,128)(2,1)} %carry_adj_tan.1, ...), custom_call_target="tpu_custom_call" | custom-call | tf_op jit(solution)/shard_map/relay/pallas_call | solution.py:676
  43.3 4.1 %deliver.1 = (bf16[1,8,2304]{2,1,0:T(8,128)(2,1)}, bf16[1,8,2304]{2,1,0:T(8,128)(2,1)}, bf16[1,8,2304]{2,1,0:T(8,128)(2,1)}, bf16[1,8,2304]{2,1,0:T(8,128)(2,1)}...) custom-call(bf16[4,8,2304]{2,1,0:T(8,128)(2,1)S(1)} %get-tuple-element.9.final, ...), custom_call_target="tpu_custom_call" | custom-call | tf_op jit(solution)/shard_map/deliver/pallas_call | solution.py:733
